TPU v7x, 32 devices: a whole 2x2x4 slice. The times are simulated.
32 devices in a mesh: grp: 2 (over y), row: 4 (over x, core), col: 4 (over z).
Axes of the slice: x: 2, y: 2, z: 4, core: 2. Of those that a mesh axis runs over, the one named last changes fastest.
Arguments:
- perturbation: bfloat16 [4, 12000, 12000], P('grp', 'row', 'col'), parts along dimension 0, may hold values from -96 to 96
- occ_coeffs: bfloat16 [12000, 2000], P('row', 'col'), may hold values from -0.0546875 to 0.0546875
- vir_coeffs: bfloat16 [12000, 512], P('col', 'row'), may hold values from -0.0546875 to 0.0546875
- occ_energies: float32 [2000], replicated, may hold values from -1 to -0.1
- vir_energies: float32 [512], replicated, may hold values from 0.1 to 1.5
Outputs:
- density_response: bfloat16 [4, 12000, 12000], P('grp', 'row', 'col'), parts along dimension 0
There are 2 independent parts, one for each index of `grp`. A program takes and returns all parts, laid end to end along the dimension named above; an argument that names none is the same for every part. Nothing has to cross between parts.
All inputs are finite; a program needn't handle non-finite values.
Results may differ from a plain program's by a relative error of at most 0.0098.
Values may be sent and summed in bfloat16 or wider, within the bound.
A program may use at most 192 MiB of HBM per device.

v0:
```python
import jax
import jax.numpy as jnp
from jax import lax
from jax.sharding import PartitionSpec as P

BF16 = jnp.bfloat16
F32 = jnp.float32


def per_device(perturbation, occ_coeffs, vir_coeffs, occ_energies, vir_energies):
    vir_rows = lax.all_gather(vir_coeffs, "row", axis=1, tiled=True)
    occ_parts = lax.all_gather(occ_coeffs, "col")
    cols, _, width = occ_parts.shape
    image = jnp.einsum("pij,jv->piv", perturbation, vir_rows, preferred_element_type=F32).astype(
        BF16
    )
    part = jnp.einsum("cio,piv->pcov", occ_parts, image, preferred_element_type=F32).astype(BF16)
    coupling = lax.psum(part, ("row", "col"))
    gaps = occ_energies.reshape(cols, width)[:, :, None] - vir_energies[None, None, :]
    response = (coupling.astype(F32) / gaps[None]).astype(BF16)
    mixed = jnp.einsum("cio,pcov->piv", occ_parts, response, preferred_element_type=F32).astype(
        BF16
    )
    return jnp.einsum("piv,jv->pij", mixed, vir_rows, preferred_element_type=F32).astype(BF16)


def solution(mesh):
    placed = (P("grp", "row", "col"), P("row", "col"), P("col", "row"), P(), P())
    return jax.shard_map(
        per_device, mesh=mesh, in_specs=placed, out_specs=P("grp", "row", "col"), check_vma=False
    )
```

profile of v0, /device:TPU:0, one launch (start us, length us, event | category | flops | bytes accessed | tf_op | source)
XLA Modules:
  0.0 448.0 jit_solution(10581064769501468559)
XLA Ops:
  6.5 0.0 all-gather.4.cloned.1.call-start
  6.5 0.7 all-gather.4.cloned.1.call-update
  7.3 0.0 all-gather.6.cloned.1.call-start
  7.3 0.7 all-gather.6.cloned.1.call-update
  8.0 0.0 all-reduce.2.cloned.1.call-start
  8.1 32.1 %all-gather.4.cloned.1.call-done = bf16[3000,512]{1,0:T(8,128)(2,1)} async-done(((bf16[3000,128]{1,0:T(8,128)(2,1)}), bf16[3000,512]{1,0:T(8,128)(2,1)}) %all-gather.4.cloned.1.call-update) | async-done | bytes 3072016 | tf_op jit(solution)/shard_map/all_gather | solution.py:11
  40.1 25.8 %fusion.45 = bf16[2,3000,512,1]{2,1,3,0:T(8,128)(2,1)} fusion(bf16[2,3000,3000]{2,1,0:T(8,128)(2,1)} %param.5, bf16[3000,512]{1,0:T(8,128)(2,1)} %all-gather.4.cloned.1.call-done), kind=kOutput, calls=%fused_computation.5.clone.clone.clone.1 | convolution fusion | flops 18435072000 | bytes 45216000 | tf_op jit(solution)/shard_map/pij,jv->piv/dot_general | solution.py:14
  66.0 189.1 %all-gather.6.cloned.1.call-done = bf16[12000,500]{1,0:T(8,128)(2,1)} async-done(((bf16[3000,500]{1,0:T(8,128)(2,1)}), bf16[12000,500]{1,0:T(8,128)(2,1)}) %all-gather.6.cloned.1.call-update) | async-done | bytes 12000016 | tf_op jit(solution)/shard_map/all_gather | solution.py:12
  255.1 19.1 %fusion.17 = bf16[2,512,4,500]{1,3,2,0:T(8,128)(2,1)} fusion(bf16[4,3000,500,1]{2,1,0,3:T(8,128)(2,1)} %bitcast.58, bf16[2,3000,512,1]{2,1,3,0:T(8,128)(2,1)} %fusion.45), kind=kOutput, calls=%fused_computation.12 | convolution fusion | flops 12290048000 | bytes 22240000 | tf_op jit(solution)/shard_map/cio,piv->pcov/dot_general | solution.py:17
  274.2 0.0 copy-start
  274.2 0.0 copy-start.1
  274.2 7.8 %copy.10 = bf16[2,512,4,500]{3,2,1,0:T(4,128)(2,1)} copy(bf16[2,512,4,500]{1,3,2,0:T(8,128)(2,1)} %fusion.17) | data formatting | bytes 8192000
  282.0 0.0 all-reduce.2.cloned.1.call-update
  282.0 0.0 copy-done
  282.1 0.1 sub.19
  282.1 0.0 copy-done.1
  282.1 2.8 broadcast_subtract_fusion
  285.0 106.6 %all-reduce.2.cloned.1.call-done = bf16[2,4,500,512]{2,1,3,0:T(4,128)(2,1)} async-done(((bf16[2,4,500,512]{2,1,3,0:T(4,128)(2,1)}), bf16[2,4,500,512]{2,1,3,0:T(4,128)(2,1)}) %all-reduce.2.cloned.1.call-update) | async-done | bytes 4096016 | tf_op jit(solution)/shard_map/psum | solution.py:18
  391.5 5.5 %fusion = bf16[2,4,500,512]{2,1,3,0:T(4,128)(2,1)S(1)} fusion(bf16[2,4,500,512]{2,1,3,0:T(4,128)(2,1)} %all-reduce.2.cloned.1.call-done, f32[4,500,512]{1,0,2:T(4,128)} %broadcast_subtract_fusion), kind=kLoop, calls=%fused_computation.3 | loop fusion | flops 6144000 | bytes 12288000 | tf_op jit(solution)/shard_map/convert_element_type | solution.py:20
  397.1 16.8 %fusion.41 = bf16[2,3000,512]{2,1,0:T(8,128)(2,1)} fusion(bf16[4,3000,500,1]{2,1,0,3:T(8,128)(2,1)} %bitcast.59, bf16[2,4,500,512]{2,1,3,0:T(4,128)(2,1)S(1)} %fusion), kind=kOutput, calls=%fused_computation.6.clone.1 | convolution fusion | flops 12291072000 | bytes 22240000 | tf_op jit(solution)/shard_map/cio,pcov->piv/dot_general | solution.py:21
  413.9 27.6 %convolution_convert_fusion = bf16[2,3000,3000]{2,1,0:T(8,128)(2,1)} fusion(bf16[3000,512]{1,0:T(8,128)(2,1)} %all-gather.4.cloned.1.call-done, bf16[2,3000,512]{2,1,0:T(8,128)(2,1)} %fusion.41), kind=kOutput, calls=%fused_computation | convolution fusion | flops 18449999872 | bytes 45216000 | tf_op jit(solution)/shard_map/piv,jv->pij/dot_general | solution.py:24
Async XLA Ops:
  6.5 33.6 %all-gather.4.cloned.1.call-start = ((), (), s32[]{:S(2)}) async-start(), calls=%async_computation | async-start | bytes 3840000 | tf_op jit(solution)/shard_map/all_gather | solution.py:11
  7.3 247.8 %all-gather.6.cloned.1.call-start = ((), (), s32[]{:S(2)}) async-start(), calls=%async_computation.2 | async-start | bytes 15360000 | tf_op jit(solution)/shard_map/all_gather | solution.py:12
  8.0 383.5 %all-reduce.2.cloned.1.call-start = ((), (), s32[]{:S(2)}) async-start(), calls=%async_computation.1 | async-start | bytes 8388608 | tf_op jit(solution)/shard_map/psum | solution.py:18
  274.2 7.9 %copy-start = (f32[2000]{0:T(1024)S(1)}, f32[2000]{0:T(1024)}, u32[]{:S(2)}) copy-start(f32[2000]{0:T(1024)} %param.8) | copy-start | bytes 24004
  274.2 8.0 %copy-start.1 = (f32[512]{0:T(512)S(1)}, f32[512]{0:T(512)}, u32[]{:S(2)}) copy-start(f32[512]{0:T(512)} %param.9) | copy-start | bytes 6148
Sparse Core Ops, SparseCore 0:
  8.9 31.1 all-gather.3
  41.7 213.3 all-gather.5
  282.2 109.3 all-reduce.1
where the time goes:
time: 448 us
  waiting for transfers between devices  329 us (73%)
  matrix products  89.4 us (20%)
  between operations  13.1 us (3%)
  other arithmetic  8.38 us (2%)
  local copies, waits for them, and re-layouts  7.93 us (2%)
    all_gather x1, waiting for transfers between devices, per_device(): occ_parts = lax.all_gather(occ_coeffs, 'col')  189 us
    psum x1, waiting for transfers between devices, per_device(): coupling = lax.psum(part, ('row', 'col'))  107 us
    all_gather x1, waiting for transfers between devices, per_device(): vir_rows = lax.all_gather(vir_coeffs, 'row', axis=1, tiled=True)  32.1 us
    dot_general x1, matrix products, per_device(): jnp.einsum('piv,jv->pij', mixed, vir_rows, preferred_element_type=F32)  27.6 us
    dot_general x1, matrix products, per_device(): jnp.einsum('pij,jv->piv', perturbation, vir_rows, preferred_element_type=...  25.8 us
    dot_general x1, matrix products, per_device(): jnp.einsum('cio,piv->pcov', occ_parts, image, preferred_element_type=F32)  19.1 us
    dot_general x1, matrix products, per_device(): jnp.einsum('cio,pcov->piv', occ_parts, response, preferred_element_type=F32)  16.8 us
  transfers between devices with their start and end apart: 3, of which 3 were waited for; matrix products, arithmetic and copies ran while one was open for 6% of the time, Pallas kernels for 0%

commit v1 on v0

--- a/solution.py
+++ b/solution.py
@@ -7,8 +7,18 @@
 F32 = jnp.float32
 
 
+def gather_by_hops(x, axis, d):
+    peers = lax.axis_size(axis)
+    current, blocks = (x, [x])
+    for _ in range(peers - 1):
+        current = lax.ppermute(current, axis, [(i, (i + 1) % peers) for i in range(peers)])
+        blocks.insert(0, current)
+    merged = jnp.concatenate(blocks, axis=d)
+    return jnp.roll(merged, (lax.axis_index(axis) + 1) * x.shape[d], axis=d)
+
+
 def per_device(perturbation, occ_coeffs, vir_coeffs, occ_energies, vir_energies):
-    vir_rows = lax.all_gather(vir_coeffs, "row", axis=1, tiled=True)
+    vir_rows = gather_by_hops(vir_coeffs, "row", 1)
     occ_parts = lax.all_gather(occ_coeffs, "col")
     cols, _, width = occ_parts.shape
     image = jnp.einsum("pij,jv->piv", perturbation, vir_rows, preferred_element_type=F32).astype(

time: 448 us -> 416 us (0.929)
  waiting for transfers between devices: 329 us -> 272 us
  local copies, waits for them, and re-layouts: 7.93 us -> 34.5 us
  matrix products: 89.4 us -> 84.6 us
    all_gather x1, waiting for transfers between devices: 189 us -> 133 us  [per_device(): occ_parts = lax.all_gather(occ_coeffs, 'col')]
    ppermute x0 -> x3, waiting for transfers between devices: none -> 34 us  [gather_by_hops(): lax.ppermute(current, axis, [(i, (i + 1) % peers) for i in range(peers)])]
    all_gather x1 -> x0, waiting for transfers between devices: 32.1 us -> none  [per_device(): vir_rows = lax.all_gather(vir_coeffs, 'row', axis=1, tiled=True)]
    unnamed x5 -> x15, local copies, waits for them, and re-layouts: 7.85 us -> 31.1 us
    dot_general x1 -> x0, matrix products: 16.8 us -> none  [per_device(): jnp.einsum('cio,pcov->piv', occ_parts, response, preferred_element_type=F32)]
    dot_general x1, matrix products: 27.6 us -> 39.1 us  [per_device(): jnp.einsum('piv,jv->pij', mixed, vir_rows, preferred_element_type=F32)]
  transfers between devices with their start and end apart: 3 -> 5, of which waited for: 3 -> 5; matrix products, arithmetic and copies ran while one was open for 6% -> 13% of each run, Pallas kernels for 0% -> 0%
where the time goes in v1:
time: 416 us
  waiting for transfers between devices  272 us (65%)
  matrix products  84.6 us (20%)
  local copies, waits for them, and re-layouts  34.5 us (8%)
  between operations  13.4 us (3%)
  other arithmetic  10.6 us (3%)
    all_gather x1, waiting for transfers between devices, per_device(): occ_parts = lax.all_gather(occ_coeffs, 'col')  133 us
    psum x1, waiting for transfers between devices, per_device(): coupling = lax.psum(part, ('row', 'col'))  104 us
    dot_general x1, matrix products, per_device(): jnp.einsum('piv,jv->pij', mixed, vir_rows, preferred_element_type=F32)  39.1 us
    ppermute x3, waiting for transfers between devices, gather_by_hops(): lax.ppermute(current, axis, [(i, (i + 1) % peers) for i in range(peers)])  34 us
    unnamed x15, local copies, waits for them, and re-layouts  31.1 us
    dot_general x1, matrix products, per_device(): jnp.einsum('pij,jv->piv', perturbation, vir_rows, preferred_element_type=...  25.6 us
    dot_general x1, matrix products, per_device(): jnp.einsum('cio,piv->pcov', occ_parts, image, preferred_element_type=F32)  20 us
  transfers between devices with their start and end apart: 5, of which 5 were waited for; matrix products, arithmetic and copies ran while one was open for 13% of the time, Pallas kernels for 0%

profile of v1, /device:TPU:0, one launch (start us, length us, event | category | flops | bytes accessed | tf_op | source)
XLA Modules:
  0.0 415.8 jit_solution(15590853100193963281)
XLA Ops:
  6.5 0.0 copy-start
  6.5 0.0 all-gather.3.cloned.1.call-start
  6.5 0.7 all-gather.3.cloned.1.call-update
  7.3 0.0 all-reduce.2.cloned.1.call-start
  7.3 0.5 collective-permute-start
  7.8 11.6 %collective-permute-done = bf16[3000,128]{1,0:T(8,128)(2,1)S(1)} collective-permute-done((bf16[3000,128]{1,0:T(8,128)(2,1)}, bf16[3000,128]{1,0:T(8,128)(2,1)S(1)}, u32[]{:S(2)}, u32[]{:S(2)}) %collective-permute-start) | collective-permute-done | bytes 768032 | tf_op jit(solution)/shard_map/ppermute | solution.py:14
  19.4 0.0 collective-permute-start.1
  19.5 11.2 %collective-permute-done.1 = bf16[3000,128]{1,0:T(8,128)(2,1)S(1)} collective-permute-done((bf16[3000,128]{1,0:T(8,128)(2,1)S(1)}, bf16[3000,128]{1,0:T(8,128)(2,1)S(1)}, u32[]{:S(2)}, u32[]{:S(2)}) %collective-permute-start.1) | collective-permute-done | bytes 768032 | tf_op jit(solution)/shard_map/ppermute | solution.py:14
  30.7 0.0 collective-permute-start.2
  30.7 11.2 %collective-permute-done.2 = bf16[3000,128]{1,0:T(8,128)(2,1)S(1)} collective-permute-done((bf16[3000,128]{1,0:T(8,128)(2,1)S(1)}, bf16[3000,128]{1,0:T(8,128)(2,1)S(1)}, u32[]{:S(2)}, u32[]{:S(2)}) %collective-permute-start.2) | collective-permute-done | bytes 768032 | tf_op jit(solution)/shard_map/ppermute | solution.py:14
  41.9 1.0 constant_dynamic-update-slice_fusion.7
  42.9 1.0 constant_dynamic-update-slice_fusion.6
  43.9 0.9 constant_dynamic-update-slice_fusion.5
  44.8 0.0 copy-done
  44.8 1.0 constant_dynamic-update-slice_fusion.4
  45.8 1.0 constant_dynamic-update-slice_fusion.3
  46.8 1.0 constant_dynamic-update-slice_fusion.2
  47.8 1.0 constant_dynamic-update-slice_fusion.1
  48.8 1.0 constant_dynamic-update-slice_fusion
  49.8 25.6 %convolution_convert_fusion.1 = bf16[512,2,3000]{0,2,1:T(8,128)(2,1)} fusion(bf16[2,3000,3000]{2,1,0:T(8,128)(2,1)} %param.5, bf16[3000,1024]{1,0:T(8,128)(2,1)} %constant_dynamic-update-slice_fusion, s32[]{:T(128)S(6)} %select_n.14), kind=kOutput, calls=%fused_computation.7 | convolution fusion | flops 18435072000 | bytes 46080004 | tf_op jit(solution)/shard_map/pij,jv->piv/dot_general | solution.py:24
  75.3 16.3 %copy.11 = bf16[512,2,3000]{2,1,0:T(2,128)(2,1)} copy(bf16[512,2,3000]{0,2,1:T(8,128)(2,1)} %convolution_convert_fusion.1) | data formatting | bytes 12288000
  91.7 133.3 %all-gather.3.cloned.1.call-done = bf16[12000,500]{1,0:T(8,128)(2,1)} async-done(((bf16[3000,500]{1,0:T(8,128)(2,1)}), bf16[12000,500]{1,0:T(8,128)(2,1)}) %all-gather.3.cloned.1.call-update) | async-done | bytes 12000016 | tf_op jit(solution)/shard_map/all_gather | solution.py:22
  225.0 20.0 %fusion.13 = bf16[2,512,4,500]{1,3,2,0:T(8,128)(2,1)} fusion(bf16[4,3000,500,1]{2,1,0,3:T(8,128)(2,1)} %bitcast.41, bf16[2,3000,512,1]{1,0,2,3:T(2,128)(2,1)} %bitcast.40), kind=kOutput, calls=%fused_computation.13 | convolution fusion | flops 12290048000 | bytes 22240000 | tf_op jit(solution)/shard_map/cio,piv->pcov/dot_general | solution.py:27
  245.0 0.0 copy-start.1
  245.0 0.0 copy-start.2
  245.0 7.8 %copy.12 = bf16[2,512,4,500]{3,2,1,0:T(4,128)(2,1)} copy(bf16[2,512,4,500]{1,3,2,0:T(8,128)(2,1)} %fusion.13) | data formatting | bytes 8192000
  252.9 0.0 all-reduce.2.cloned.1.call-update
  252.9 0.0 copy-done.1
  252.9 0.1 sub.24
  253.0 0.0 copy-done.2
  253.0 3.1 broadcast_subtract_fusion
  256.1 2.3 fusion.33
  258.4 104.0 %all-reduce.2.cloned.1.call-done = bf16[2,4,500,512]{2,1,3,0:T(4,128)(2,1)} async-done(((bf16[2,4,500,512]{2,1,3,0:T(4,128)(2,1)}), bf16[2,4,500,512]{2,1,3,0:T(4,128)(2,1)}) %all-reduce.2.cloned.1.call-update) | async-done | bytes 4096016 | tf_op jit(solution)/shard_map/psum | solution.py:28
  362.4 7.5 %fusion = bf16[2,4,500,512]{2,1,3,0:T(4,128)(2,1)} fusion(bf16[2,4,500,512]{2,1,3,0:T(4,128)(2,1)} %all-reduce.2.cloned.1.call-done, f32[4,500,512]{1,0,2:T(4,128)} %broadcast_subtract_fusion), kind=kLoop, calls=%fused_computation.3 | loop fusion | flops 6144000 | bytes 12288000 | tf_op jit(solution)/shard_map/convert_element_type | solution.py:30
  369.9 39.1 %convolution_convert_fusion = bf16[2,3000,3000]{2,1,0:T(8,128)(2,1)} fusion(bf16[4,3000,500,1]{2,1,0,3:T(8,128)(2,1)} %bitcast.42, bf16[2,4,500,512]{2,1,3,0:T(4,128)(2,1)} %fusion, bf16[3000,512,1]{1,0,2:T(8,128)(2,1)S(1)} %fusion.33), kind=kOutput, calls=%fused_computation | convolution fusion | flops 30741071872 | bytes 55168000 | tf_op jit(solution)/shard_map/piv,jv->pij/dot_general | solution.py:34
Async XLA Ops:
  6.5 38.3 %copy-start = (bf16[3000,128]{1,0:T(8,128)(2,1)S(1)}, bf16[3000,128]{1,0:T(8,128)(2,1)}, u32[]{:S(2)}) copy-start(bf16[3000,128]{1,0:T(8,128)(2,1)} %param.7) | copy-start | bytes 2304004
  6.5 218.5 %all-gather.3.cloned.1.call-start = ((), (), s32[]{:S(2)}) async-start(), calls=%async_computation.1 | async-start | bytes 15360000 | tf_op jit(solution)/shard_map/all_gather | solution.py:22
  7.3 355.2 %all-reduce.2.cloned.1.call-start = ((), (), s32[]{:S(2)}) async-start(), calls=%async_computation | async-start | bytes 8388608 | tf_op jit(solution)/shard_map/psum | solution.py:28
  7.3 12.1 %collective-permute-start = (bf16[3000,128]{1,0:T(8,128)(2,1)}, bf16[3000,128]{1,0:T(8,128)(2,1)S(1)}, u32[]{:S(2)}, u32[]{:S(2)}) collective-permute-start(bf16[3000,128]{1,0:T(8,128)(2,1)} %param.7), channel_id=1, source_target_pairs={{0,4},{4,8},{8,12},{12,0},{1,5},{5,9},{9,13},{13,1},{2,6},{6,10},{... | collective-permute-start | bytes 2304008 | tf_op jit(solution)/shard_map/ppermute | solution.py:14
  19.4 11.2 %collective-permute-start.1 = (bf16[3000,128]{1,0:T(8,128)(2,1)S(1)}, bf16[3000,128]{1,0:T(8,128)(2,1)S(1)}, u32[]{:S(2)}, u32[]{:S(2)}) collective-permute-start(bf16[3000,128]{1,0:T(8,128)(2,1)S(1)} %collective-permute-done), channel_id=1, source_target_pairs={{0,4},{4,8},{8,12},{12,0},{1,5},{5,9},{9,13},{13,1},{2,6},{6,10},{... | collective-permute-start | bytes 2304008 | tf_op jit(solution)/shard_map/ppermute | solution.py:14
  30.7 11.2 %collective-permute-start.2 = (bf16[3000,128]{1,0:T(8,128)(2,1)S(1)}, bf16[3000,128]{1,0:T(8,128)(2,1)S(1)}, u32[]{:S(2)}, u32[]{:S(2)}) collective-permute-start(bf16[3000,128]{1,0:T(8,128)(2,1)S(1)} %collective-permute-done.1), channel_id=1, source_target_pairs={{0,4},{4,8},{8,12},{12,0},{1,5},{5,9},{9,13},{13,1},{2,6},{6,10},{... | collective-permute-start | bytes 2304008 | tf_op jit(solution)/shard_map/ppermute | solution.py:14
  245.0 7.9 %copy-start.1 = (f32[2000]{0:T(1024)S(1)}, f32[2000]{0:T(1024)}, u32[]{:S(2)}) copy-start(f32[2000]{0:T(1024)} %param.8) | copy-start | bytes 24004
  245.0 8.0 %copy-start.2 = (f32[512]{0:T(512)S(1)}, f32[512]{0:T(512)}, u32[]{:S(2)}) copy-start(f32[512]{0:T(512)} %param.9) | copy-start | bytes 6148
Sparse Core Ops, SparseCore 0:
  8.9 216.0 all-gather.2
  253.0 109.3 all-reduce.1
